TPU v7x, 128 devices: a whole 4x4x4 slice. The times are simulated.
128 devices in a mesh: row: 8 (over x_hi, z), col: 16 (over x_lo, y, core).
Axes of the slice: x: 4 (x_hi: 2, x_lo: 2; x = x_hi * 2 + x_lo), y: 4, z: 4, core: 2. Of those that a mesh axis runs over, the one named last changes fastest.
Arguments:
- customer_inputs: bfloat16 [131072, 1024], P(('row', 'col')), may hold values from -6 to 6
- candidate_inputs: bfloat16 [131072, 1024], P(('row', 'col')), may hold values from -6 to 6
- affinity_sharpness: bfloat16 [131072], P(('row', 'col')), may hold values from 4 to 40
- correct_candidate_index: int32 [131072], P(('row', 'col')), may hold values from 0 to 8191
- customer_initial_weights: bfloat16 [1024, 512], replicated, may hold values from -0.1875 to 0.1875
- customer_final_weights: bfloat16 [512, 256], replicated, may hold values from -0.25 to 0.25
- candidate_initial_weights: bfloat16 [1024, 512], replicated, may hold values from -0.1875 to 0.1875
- candidate_final_weights: bfloat16 [512, 256], replicated, may hold values from -0.25 to 0.25
Outputs:
- loss: float32 [], replicated
- grad_user_first: float32 [1024, 512], replicated
- grad_user_second: float32 [512, 256], replicated
- grad_item_first: float32 [1024, 512], replicated
- grad_item_second: float32 [512, 256], replicated
Inputs may be any that keep to these rules, and one draw needn't show every extreme that they name: correct_candidate_index[u] indexes the items of u's group in the order of the steps.
All inputs are finite; a program needn't handle non-finite values.
Results may differ from a plain program's by a relative error of at most 0.015.
Values may be sent and summed in bfloat16 or wider, within the bound.
No kernel may reach another device: no remote copies, remote signals or barrier semaphores. Data moves between devices by JAX's collectives and lax.ppermute only.
A program may use at most 128 MiB of HBM per device.

v0:
```python
import jax
import jax.numpy as jnp
from jax import lax
from jax.sharding import PartitionSpec as P

EPS = 1e-06


def laid_out(tiles, dim):
    dims = list(tiles.shape[1:])
    dims[dim] *= tiles.shape[0]
    return jnp.moveaxis(tiles, 0, dim).reshape(dims)


def copy_for_each(value, axis):
    copies = jnp.broadcast_to(value, (lax.axis_size(axis), *value.shape))
    return lax.all_to_all(copies, axis, split_axis=0, concat_axis=0, tiled=True)


def gathered_copies(value, axis, dim):
    return laid_out(copy_for_each(value, axis), dim)


def tower_forward(feats, first, second):
    pre = jnp.dot(feats, first, preferred_element_type=jnp.float32)
    hidden = jax.nn.relu(pre).astype(jnp.bfloat16)
    out = jnp.dot(hidden, second, preferred_element_type=jnp.float32)
    inv = lax.rsqrt(jnp.mean(out * out, axis=-1, keepdims=True) + EPS)
    return ((out * inv).astype(jnp.bfloat16), (pre, hidden, out, inv))


def tower_backward(feats, second, saved, grad_vec):
    pre, hidden, out, inv = saved
    grad = grad_vec.astype(jnp.float32)
    normed = out * inv
    grad_out = (inv * (grad - normed * jnp.mean(grad * normed, axis=-1, keepdims=True))).astype(
        jnp.bfloat16
    )
    grad_second = jnp.dot(hidden.T, grad_out, preferred_element_type=jnp.float32)
    grad_hidden = jnp.dot(grad_out, second.T, preferred_element_type=jnp.float32)
    grad_pre = jnp.where(pre > 0, grad_hidden, 0.0).astype(jnp.bfloat16)
    grad_first = jnp.dot(feats.T, grad_pre, preferred_element_type=jnp.float32)
    return (grad_first, grad_second)


def positive_pair_logit(
    shopper_vector, gathered_entries, affinity_sharpness, correct_candidate_index, resident_table
):
    latent_code = shopper_vector.shape[-1]
    coolness_fp32_number = affinity_sharpness.astype(jnp.float32)
    affinity_matrix = (
        coolness_fp32_number[:, None]
        * jnp.einsum(
            "ue,ie->ui", shopper_vector, gathered_entries, preferred_element_type=jnp.float32
        )
        / latent_code
    )
    lse = jax.nn.logsumexp(affinity_matrix, axis=1)
    columns = lax.broadcasted_iota(jnp.int32, affinity_matrix.shape, 1)
    target_column = columns == correct_candidate_index[:, None]
    picked = jnp.sum(jnp.where(target_column, affinity_matrix, 0.0), axis=1)
    softmax_likelihood = jnp.exp(affinity_matrix - lse[:, None])
    sensitivity_of_affinities = (
        (softmax_likelihood - target_column.astype(jnp.float32))
        * (coolness_fp32_number / (latent_code * resident_table))[:, None]
    ).astype(jnp.bfloat16)
    customer_derivative = jnp.dot(
        sensitivity_of_affinities, gathered_entries, preferred_element_type=jnp.float32
    )
    return (lse, sensitivity_of_affinities, customer_derivative, jnp.sum(lse - picked))


def body(
    customer_inputs,
    candidate_inputs,
    affinity_sharpness,
    correct_candidate_index,
    customer_initial_weights,
    customer_final_weights,
    candidate_initial_weights,
    candidate_final_weights,
):
    resident_table = customer_inputs.shape[0]
    shopper_vector, user_saved = tower_forward(
        customer_inputs, customer_initial_weights, customer_final_weights
    )
    offered_thing_vector, item_saved = tower_forward(
        candidate_inputs, candidate_initial_weights, candidate_final_weights
    )
    latent_code = shopper_vector.shape[-1]
    gathered_entries = lax.all_gather(offered_thing_vector, "row", axis=0, tiled=True)
    lse, sensitivity_of_affinities, customer_derivative, loss_local = positive_pair_logit(
        shopper_vector,
        gathered_entries,
        affinity_sharpness,
        correct_candidate_index,
        resident_table,
    )
    all_users, all_scales = (
        lax.all_gather(shopper_vector, "row", axis=0, tiled=True),
        lax.all_gather(affinity_sharpness, "row", axis=0, tiled=True),
    )
    all_positive = gathered_copies(correct_candidate_index, "row", 0)
    all_lse = gathered_copies(lse, "row", 0)
    coolness_fp32_number = all_scales.astype(jnp.float32)
    affinity_matrix = (
        coolness_fp32_number[:, None]
        * jnp.einsum(
            "ue,ie->ui", all_users, offered_thing_vector, preferred_element_type=jnp.float32
        )
        / latent_code
    )
    start = lax.axis_index("row") * resident_table
    columns = lax.broadcasted_iota(jnp.int32, affinity_matrix.shape, 1) + start
    target_column = columns == all_positive[:, None]
    softmax_likelihood = jnp.exp(affinity_matrix - all_lse[:, None])
    group_dlogits = (
        (softmax_likelihood - target_column.astype(jnp.float32))
        * (coolness_fp32_number / (latent_code * resident_table))[:, None]
    ).astype(jnp.bfloat16)
    candidate_derivative = jnp.einsum(
        "ui,ue->ie", group_dlogits, all_users, preferred_element_type=jnp.float32
    )
    grad_user_first, grad_user_second = tower_backward(
        customer_inputs,
        customer_final_weights,
        user_saved,
        customer_derivative.astype(jnp.bfloat16),
    )
    grad_item_first, grad_item_second = tower_backward(
        candidate_inputs,
        candidate_final_weights,
        item_saved,
        candidate_derivative.astype(jnp.bfloat16),
    )
    summed = (
        lax.psum(grad_user_first.astype(jnp.bfloat16), ("row", "col")).astype(jnp.float32),
        lax.psum(grad_user_second.astype(jnp.bfloat16), ("row", "col")).astype(jnp.float32),
        lax.psum(grad_item_first.astype(jnp.bfloat16), ("row", "col")).astype(jnp.float32),
        lax.psum(grad_item_second.astype(jnp.bfloat16), ("row", "col")).astype(jnp.float32),
        lax.psum(loss_local.astype(jnp.bfloat16), ("row", "col")).astype(jnp.float32),
    )
    users_total = resident_table * lax.axis_size("row") * lax.axis_size("col")
    return (summed[4] / users_total, summed[0], summed[1], summed[2], summed[3])


def solution(mesh):
    placed = (
        P(("row", "col"), None),
        P(("row", "col"), None),
        P(("row", "col")),
        P(("row", "col")),
        P(),
        P(),
        P(),
        P(),
    )
    return jax.shard_map(
        body, mesh=mesh, in_specs=placed, out_specs=(P(), P(), P(), P(), P()), check_vma=False
    )
```

profile of v0, /device:TPU:1, one launch (start us, length us, event | category | flops | bytes accessed | tf_op | source)
XLA Modules:
  0.0 351.3 jit_solution(15818196188370760790)
XLA Ops:
  7.2 3.3 fusion.28
  10.5 1.3 copy-done.4
  12.4 0.9 multiply_convert_fusion.8
  13.3 0.6 broadcast_in_dim.15
  13.9 8.3 %all-to-all-start.1 = ((s32[8,1,1024]{2,1,0:T(1,128)}), s32[8,1,1024]{2,1,0:T(1,128)S(1)}, u32[]{:S(2)}, u32[]{:S(2)}) async-start(s32[8,1,1024]{2,1,0:T(1,128)} %broadcast_in_dim.15), calls=%async_computation.1 | async-start | bytes 65536 | tf_op jit(solution)/shard_map/all_to_all | solution.py:17
  22.3 2.5 fusion.27
  24.8 1.3 copy-done.6
  26.7 0.9 copy-done.2
  27.6 0.9 multiply_convert_fusion.9
  28.6 26.5 %all_gather.10 = bf16[8192]{0:T(1024)(128)(2,1)S(1)} all-gather(bf16[1024]{0:T(1024)(128)(2,1)S(1)} %copy-done.13), channel_id=1, replica_groups=mesh['row'=8,'col'=16] {'row'}, dimensions={0}, use_global_device_ids=true | all-gather | bytes 18432 | tf_op jit(solution)/shard_map/all_gather | solution.py:101
  55.1 32.1 %all-gather.3.cloned.1.call-done = bf16[8192,256]{0,1:T(8,128)(2,1)} async-done(((bf16[1024,256]{0,1:T(8,128)(2,1)}), bf16[8192,256]{0,1:T(8,128)(2,1)}) %all-gather.3.cloned.1.call-update) | async-done | bytes 4194320 | tf_op jit(solution)/shard_map/all_gather | solution.py:91
  87.2 16.0 %fusion = (f32[1024]{0:T(1024)S(1)}, f32[1024,8192]{1,0:T(8,128)}) fusion(f32[1024]{0:T(1024)S(1)} %convert_element_type.90, bf16[1024,256]{0,1:T(8,128)(2,1)} %multiply_convert_fusion.9, bf16[8192,256]{0,1:T(8,128)(2,1)} %all-gather.3.cloned.1.call-done), kind=kOutput, calls=%fused_computation.6 | convolution fusion | flops 4320132096 | bytes 38281216 | tf_op jit(solution)/shard_map/ue,ie->ui/dot_general | solution.py:53
  103.2 18.4 %select_reduce_fusion = (f32[1024]{0:T(1024)S(1)}, f32[1024]{0:T(1024)S(1)}) fusion(f32[1024,8192]{1,0:T(8,128)} %get-tuple-element.28, s32[1024]{0:T(1024)S(1)} %copy-done.14, f32[1024]{0:T(1024)S(1)} %convert_element_type.90, f32[1024]{0:T(1024)S(1)} %is-finite_select_fusion), kind=kLoop, calls=%fused_computation.2 | loop fusion | flops 58718208 | bytes 33574912 | tf_op jit(solution)/shard_map/reduce_sum | solution.py:61
  121.6 0.6 subtract_reduce_fusion
  122.3 20.4 %fusion.9 = (f32[1024]{0:T(1024)S(1)}, bf16[1024,256]{0,1:T(8,128)(2,1)S(1)}) fusion(f32[1024,256]{0,1:T(8,128)S(1)} %copy-done.3, f32[1024]{0:T(1024)S(1)} %add_rsqrt_fusion.1, bf16[8192,256]{0,1:T(8,128)(2,1)} %all-gather.3.cloned.1.call-done, f32[1024,8192]{1,0:T(8,128)} %get-tuple-element.28, f32[1024]{0:T(1024)S(1)} %broadcast_multiply_fusion.1, ...), kind=kOutput, calls=%fused_computation.26 | convolution fusion | flops 4363385856 | bytes 39346176 | tf_op jit(solution)/shard_map/dot_general | solution.py:67
  142.6 1.0 fusion.11
  143.6 4.4 %fusion.5 = bf16[1024,512]{0,1:T(8,128)(2,1)} fusion(bf16[1024,1024]{1,0:T(8,128)(2,1)S(1)} %copy-done, f32[1024,512]{1,0:T(8,128)} %copy-done.6, bf16[1024,256]{0,1:T(8,128)(2,1)} %fusion.11, bf16[512,256]{1,0:T(8,128)(2,1)S(1)} %copy-done.10), kind=kOutput, calls=%fused_computation.16 | convolution fusion | flops 1344274432 | bytes 6029312 | tf_op jit(solution)/shard_map/dot_general | solution.py:42
  148.0 0.6 broadcast_in_dim.14
  148.6 3.3 all-to-all-start
  152.0 2.9 convolution_convert_fusion.3
  154.9 4.5 %all-gather.5.cloned.1.call-done = bf16[8192,256]{0,1:T(8,128)(2,1)} async-done(((bf16[1024,256]{0,1:T(8,128)(2,1)}), bf16[8192,256]{0,1:T(8,128)(2,1)}) %all-gather.5.cloned.1.call-update) | async-done | bytes 4194320 | tf_op jit(solution)/shard_map/all_gather | solution.py:100
  159.4 14.2 %multiply_convert_fusion.5.clone.4 = bf16[8192,1024]{1,0:T(8,128)(2,1)S(1)} fusion(f32[8192]{0:T(1024)S(1)} %broadcast_multiply_fusion, s32[1024]{0:T(1024)S(1)} %iota_add_fusion, f32[8192]{0:T(1024)S(1)} %bitcast.31, f32[8192]{0:T(1024)S(1)} %convert_element_type.108, s32[8192]{0:T(1024)S(1)} %bitcast.30, ...), kind=kOutput, calls=%fused_computation.clone.clone.clone.clone.clone.clone.1 | convolution fusion | flops 4362600448 | bytes 22159360 | tf_op jit(solution)/shard_map/ue,ie->ui/dot_general | solution.py:108
  173.7 4.7 %fusion.12 = (f32[1024]{0:T(1024)S(1)}, bf16[1024,256]{0,1:T(8,128)(2,1)S(1)}) fusion(f32[1024,256]{0,1:T(8,128)S(1)} %get-tuple-element.26, f32[1024]{0:T(1024)S(1)} %add_rsqrt_fusion, bf16[8192,256]{0,1:T(8,128)(2,1)S(1)} %copy-done.15, bf16[8192,1024]{1,0:T(8,128)(2,1)S(1)} %multiply_convert_fusion.5.clone.4), kind=kOutput, calls=%fused_computation.29 | convolution fusion | flops 4296276992 | bytes 22552576 | tf_op jit(solution)/shard_map/ui,ue->ie/dot_general | solution.py:121
  178.3 1.0 fusion.14
  179.3 4.4 %fusion.6 = bf16[1024,512]{0,1:T(8,128)(2,1)} fusion(bf16[1024,1024]{1,0:T(8,128)(2,1)} %param.9, f32[1024,512]{1,0:T(8,128)S(1)} %copy-done.5, bf16[1024,256]{0,1:T(8,128)(2,1)} %fusion.14, bf16[512,256]{1,0:T(8,128)(2,1)S(1)} %copy-done.12), kind=kOutput, calls=%fused_computation.17 | convolution fusion | flops 1344274432 | bytes 6029312 | tf_op jit(solution)/shard_map/dot_general | solution.py:42
  183.7 1.2 convolution_convert_fusion.2
  185.0 64.6 %psum.35 = bf16[]{:T(256)} all-reduce(bf16[]{:T(256)} %get-tuple-element.21), channel_id=1, replica_groups=mesh['row'=8,'col'=16] {'row','col'}, use_global_device_ids=true, to_apply=%region_6.7 | all-reduce | flops 1 | bytes 4 | tf_op jit(solution)/shard_map/psum | solution.py:141
  250.2 86.5 %all-reduce.3.cloned.1.call-done = (bf16[1024,512]{0,1:T(8,128)(2,1)}, bf16[1024,512]{0,1:T(8,128)(2,1)}, bf16[512,256]{1,0:T(8,128)(2,1)}, bf16[512,256]{1,0:T(8,128)(2,1)}) async-done(((bf16[1024,512]{0,1:T(8,128)(2,1)}, bf16[1024,512]{0,1:T(8,128)(2,1)}, bf16[512,256]{1,0:T(8,128)(2,1)}, bf16[512,256]{1,0:T(8,128)(2,1)}), (bf16[1024,512]{0,1:T(8,128)(2,1)}, bf16[1024,512]{0,1:T(8,128)(2,1)}, ...) | async-done | bytes 2621456 | tf_op jit(solution)/shard_map/psum | solution.py:137
  336.8 2.7 copy.15
  339.5 1.8 convert_element_type.107
  341.2 1.6 copy.16
  342.8 0.8 convert_element_type.119
  (49 shorter events, 1.3 us)
Async XLA Ops:
  7.2 15.1 %copy-start = (bf16[1024,1024]{1,0:T(8,128)(2,1)S(1)}, bf16[1024,1024]{1,0:T(8,128)(2,1)}, u32[]{:S(2)}) copy-start(bf16[1024,1024]{1,0:T(8,128)(2,1)} %param.8) | copy-start | bytes 6291460
  7.2 4.7 %copy-start.11 = (bf16[512,256]{1,0:T(8,128)(2,1)S(1)}, bf16[512,256]{1,0:T(8,128)(2,1)}, u32[]{:S(2)}) copy-start(bf16[512,256]{1,0:T(8,128)(2,1)} %param.15) | copy-start | bytes 786436
  7.2 80.0 %all-gather.3.cloned.1.call-start = ((), (), s32[]{:S(2)}) async-start(), calls=%async_computation.2 | async-start | bytes 4718592 | tf_op jit(solution)/shard_map/all_gather | solution.py:91
  10.5 1.3 copy-start.4
  11.8 1.4 copy-start.14
  13.9 134.1 %all-to-all-start.1 = ((s32[8,1,1024]{2,1,0:T(1,128)}), s32[8,1,1024]{2,1,0:T(1,128)S(1)}, u32[]{:S(2)}, u32[]{:S(2)}) async-start(s32[8,1,1024]{2,1,0:T(1,128)} %broadcast_in_dim.15), calls=%async_computation.1 | async-start | bytes 65536 | tf_op jit(solution)/shard_map/all_to_all | solution.py:17
  22.2 3.9 %copy-start.10 = (bf16[512,256]{1,0:T(8,128)(2,1)S(1)}, bf16[512,256]{1,0:T(8,128)(2,1)}, u32[]{:S(2)}) copy-start(bf16[512,256]{1,0:T(8,128)(2,1)} %param.13) | copy-start | bytes 786436
  22.2 137.2 %all-gather.5.cloned.1.call-start = ((), (), s32[]{:S(2)}) async-start(), calls=%async_computation.3 | async-start | bytes 4718592 | tf_op jit(solution)/shard_map/all_gather | solution.py:100
  24.8 1.3 copy-start.6
  26.1 2.4 copy-start.13
  26.6 1.0 copy-start.2
  103.2 19.0 %copy-start.3 = (f32[1024,256]{0,1:T(8,128)S(1)}, f32[1024,256]{0,1:T(8,128)}, u32[]{:S(2)}) copy-start(f32[1024,256]{0,1:T(8,128)} %copy-done.2) | copy-start | bytes 3145732
  148.6 10.8 %all-to-all-start = ((f32[8,1,1024]{2,1,0:T(1,128)}), f32[8,1,1024]{2,1,0:T(1,128)S(1)}, u32[]{:S(2)}, u32[]{:S(2)}) async-start(f32[8,1,1024]{2,1,0:T(1,128)} %broadcast_in_dim.14), calls=%async_computation | async-start | bytes 65536 | tf_op jit(solution)/shard_map/all_to_all | solution.py:17
  152.0 184.8 %all-reduce.3.cloned.1.call-start = ((), (), s32[]{:S(2)}) async-start(), calls=%async_computation.4 | async-start | bytes 5242880 | tf_op jit(solution)/shard_map/psum | solution.py:137
  159.4 14.2 %copy-start.15 = (bf16[8192,256]{0,1:T(8,128)(2,1)S(1)}, bf16[8192,256]{0,1:T(8,128)(2,1)}, u32[]{:S(2)}) copy-start(bf16[8192,256]{0,1:T(8,128)(2,1)} %all-gather.5.cloned.1.call-done) | copy-start | bytes 12582916
  173.6 5.7 %copy-start.5 = (f32[1024,512]{1,0:T(8,128)S(1)}, f32[1024,512]{1,0:T(8,128)}, u32[]{:S(2)}) copy-start(f32[1024,512]{1,0:T(8,128)} %copy-done.4) | copy-start | bytes 6291460
  173.6 5.7 %copy-start.12 = (bf16[512,256]{1,0:T(8,128)(2,1)S(1)}, bf16[512,256]{1,0:T(8,128)(2,1)}, u32[]{:S(2)}) copy-start(bf16[512,256]{1,0:T(8,128)(2,1)} %param.15) | copy-start | bytes 786436
  179.3 4.4 %copy-start.7 = (bf16[1024,256]{0,1:T(8,128)(2,1)S(1)}, bf16[1024,256]{0,1:T(8,128)(2,1)}, u32[]{:S(2)}) copy-start(bf16[1024,256]{0,1:T(8,128)(2,1)} %fusion.14) | copy-start | bytes 1572868
  185.0 158.7 %copy-start.1 = (bf16[1024,1024]{1,0:T(8,128)(2,1)S(1)}, bf16[1024,1024]{1,0:T(8,128)(2,1)}, u32[]{:S(2)}) copy-start(bf16[1024,1024]{1,0:T(8,128)(2,1)} %param.8) | copy-start | bytes 6291460
  336.8 4.5 %copy-start.8 = (bf16[1024,512]{0,1:T(8,128)(2,1)S(1)}, bf16[1024,512]{0,1:T(8,128)(2,1)}, u32[]{:S(2)}) copy-start(bf16[1024,512]{0,1:T(8,128)(2,1)} %get-tuple-element.18) | copy-start | bytes 3145732
  336.8 6.1 %copy-start.9 = (bf16[512,256]{1,0:T(8,128)(2,1)S(1)}, bf16[512,256]{1,0:T(8,128)(2,1)}, u32[]{:S(2)}) copy-start(bf16[512,256]{1,0:T(8,128)(2,1)} %get-tuple-element.20) | copy-start | bytes 786436
Sparse Core Ops, SparseCore 0:
  13.4 73.7 all-gather.2
  90.1 69.2 all-gather.4
  185.1 151.6 all-reduce.2
where the time goes:
time: 352 us; the launch traced here: 351 us
  waiting for transfers between devices  123 us (35%)
  blocking collectives  91.1 us (26%)
  matrix products  74.8 us (21%)
  other arithmetic  25.5 us (7%)
  between operations  15.8 us (4%)
  starting transfers between devices  11.8 us (3%)
  local copies, waits for them, and re-layouts  9.18 us (3%)
    psum x1, waiting for transfers between devices, body(): lax.psum(grad_user_first.astype(jnp.bfloat16), ('row', 'col'))  86.5 us
    psum x1, blocking collectives, body(): lax.psum(loss_local.astype(jnp.bfloat16), ('row', 'col'))  64.6 us
    all_gather x1, waiting for transfers between devices, body(): lax.all_gather(offered_thing_vector, 'row', axis=0, tiled=True)  32.1 us
    all_gather x1, blocking collectives, body(): lax.all_gather(affinity_sharpness, 'row', axis=0, tiled=True)  26.5 us
    dot_general x1, matrix products, positive_pair_logit(): jnp.dot(sensitivity_of_affinities, gathered_entries, preferred_element_ty...  20.4 us
    reduce_sum x1, other arithmetic, positive_pair_logit(): picked = jnp.sum(jnp.where(target_column, affinity_matrix, 0.0), axis=1)  18.4 us
    dot_general x1, matrix products, positive_pair_logit(): jnp.einsum('ue,ie->ui', shopper_vector, gathered_entries, preferred_eleme...  16 us
    dot_general x1, matrix products, body(): jnp.einsum('ue,ie->ui', all_users, offered_thing_vector, preferred_elemen...  14.2 us
  transfers between devices with their start and end apart: 5, of which 3 were waited for; matrix products, arithmetic and copies ran while one was open for 20% of the time, Pallas kernels for 0%

commit v1 on v0

--- a/solution.py
+++ b/solution.py
@@ -134,7 +134,7 @@
         candidate_derivative.astype(jnp.bfloat16),
     )
     summed = (
-        lax.psum(grad_user_first.astype(jnp.bfloat16), ("row", "col")).astype(jnp.float32),
+        lax.psum(lax.psum(grad_user_first.astype(jnp.bfloat16), "col"), "row").astype(jnp.float32),
         lax.psum(grad_user_second.astype(jnp.bfloat16), ("row", "col")).astype(jnp.float32),
         lax.psum(grad_item_first.astype(jnp.bfloat16), ("row", "col")).astype(jnp.float32),
         lax.psum(grad_item_second.astype(jnp.bfloat16), ("row", "col")).astype(jnp.float32),

time: 352 us -> 537 us (1.53)
  waiting for transfers between devices: 123 us -> 298 us
    psum x1 -> x3, waiting for transfers between devices: 86.5 us -> 261 us  [the longest x1 95.5 us: body(): lax.psum(grad_user_first.astype(jnp.bfloat16), 'col')]
  transfers between devices with their start and end apart: 5 -> 7, of which waited for: 3 -> 5; matrix products, arithmetic and copies ran while one was open for 20% -> 19% of each run, Pallas kernels for 0% -> 0%
where the time goes in v1:
time: 537 us; the launch traced here: 531 us
  waiting for transfers between devices  298 us (55%)
  blocking collectives  94.4 us (18%)
  matrix products  74.8 us (14%)
  other arithmetic  25.6 us (5%)
  between operations  15.8 us (3%)
  starting transfers between devices  11.8 us (2%)
  local copies, waits for them, and re-layouts  10.8 us (2%)
    psum x1, waiting for transfers between devices, body(): lax.psum(grad_user_first.astype(jnp.bfloat16), 'col')  95.5 us
    psum x1, waiting for transfers between devices, body(): lax.psum(grad_item_first.astype(jnp.bfloat16), ('row', 'col'))  88.4 us
    psum x1, waiting for transfers between devices, body(): lax.psum(lax.psum(grad_user_first.astype(jnp.bfloat16), 'col'), 'row')  77.3 us
    psum x1, blocking collectives, body(): lax.psum(loss_local.astype(jnp.bfloat16), ('row', 'col'))  67.8 us
    all_gather x1, waiting for transfers between devices, body(): lax.all_gather(offered_thing_vector, 'row', axis=0, tiled=True)  32.1 us
    all_gather x1, blocking collectives, body(): lax.all_gather(affinity_sharpness, 'row', axis=0, tiled=True)  26.5 us
    dot_general x1, matrix products, positive_pair_logit(): jnp.dot(sensitivity_of_affinities, gathered_entries, preferred_element_ty...  20.4 us
    reduce_sum x1, other arithmetic, positive_pair_logit(): picked = jnp.sum(jnp.where(target_column, affinity_matrix, 0.0), axis=1)  18.4 us
  transfers between devices with their start and end apart: 7, of which 5 were waited for; matrix products, arithmetic and copies ran while one was open for 19% of the time, Pallas kernels for 0%

profile of v1, /device:TPU:1, one launch (start us, length us, event | category | flops | bytes accessed | tf_op | source)
XLA Modules:
  0.0 531.0 jit_solution(14344625796249512213)
XLA Ops:
  7.2 3.3 fusion.28
  10.5 1.3 copy-done.4
  12.4 0.9 multiply_convert_fusion.8
  13.3 0.6 broadcast_in_dim.15
  13.9 8.3 %all-to-all-start.1 = ((s32[8,1,1024]{2,1,0:T(1,128)}), s32[8,1,1024]{2,1,0:T(1,128)S(1)}, u32[]{:S(2)}, u32[]{:S(2)}) async-start(s32[8,1,1024]{2,1,0:T(1,128)} %broadcast_in_dim.15), calls=%async_computation.1 | async-start | bytes 65536 | tf_op jit(solution)/shard_map/all_to_all | solution.py:17
  22.3 2.5 fusion.27
  24.8 1.3 copy-done.6
  26.7 0.9 copy-done.2
  27.6 0.9 multiply_convert_fusion.9
  28.5 26.5 %all_gather.10 = bf16[8192]{0:T(1024)(128)(2,1)S(1)} all-gather(bf16[1024]{0:T(1024)(128)(2,1)S(1)} %copy-done.11), channel_id=1, replica_groups=mesh['row'=8,'col'=16] {'row'}, dimensions={0}, use_global_device_ids=true | all-gather | bytes 18432 | tf_op jit(solution)/shard_map/all_gather | solution.py:101
  55.1 32.1 %all-gather.3.cloned.1.call-done = bf16[8192,256]{0,1:T(8,128)(2,1)} async-done(((bf16[1024,256]{0,1:T(8,128)(2,1)}), bf16[8192,256]{0,1:T(8,128)(2,1)}) %all-gather.3.cloned.1.call-update) | async-done | bytes 4194320 | tf_op jit(solution)/shard_map/all_gather | solution.py:91
  87.2 16.0 %fusion = (f32[1024]{0:T(1024)S(1)}, f32[1024,8192]{1,0:T(8,128)}) fusion(f32[1024]{0:T(1024)S(1)} %convert_element_type.90, bf16[1024,256]{0,1:T(8,128)(2,1)} %multiply_convert_fusion.9, bf16[8192,256]{0,1:T(8,128)(2,1)} %all-gather.3.cloned.1.call-done), kind=kOutput, calls=%fused_computation.6 | convolution fusion | flops 4320132096 | bytes 38281216 | tf_op jit(solution)/shard_map/ue,ie->ui/dot_general | solution.py:53
  103.2 18.4 %select_reduce_fusion = (f32[1024]{0:T(1024)S(1)}, f32[1024]{0:T(1024)S(1)}) fusion(f32[1024,8192]{1,0:T(8,128)} %get-tuple-element.27, s32[1024]{0:T(1024)S(1)} %copy-done.12, f32[1024]{0:T(1024)S(1)} %convert_element_type.90, f32[1024]{0:T(1024)S(1)} %is-finite_select_fusion), kind=kLoop, calls=%fused_computation.2 | loop fusion | flops 58718208 | bytes 33574912 | tf_op jit(solution)/shard_map/reduce_sum | solution.py:61
  122.3 20.4 %fusion.9 = (f32[1024]{0:T(1024)S(1)}, bf16[1024,256]{0,1:T(8,128)(2,1)S(1)}) fusion(f32[1024,256]{0,1:T(8,128)S(1)} %copy-done.3, f32[1024]{0:T(1024)S(1)} %add_rsqrt_fusion.1, bf16[8192,256]{0,1:T(8,128)(2,1)} %all-gather.3.cloned.1.call-done, f32[1024,8192]{1,0:T(8,128)} %get-tuple-element.27, f32[1024]{0:T(1024)S(1)} %broadcast_multiply_fusion.1, ...), kind=kOutput, calls=%fused_computation.26 | convolution fusion | flops 4363385856 | bytes 39346176 | tf_op jit(solution)/shard_map/dot_general | solution.py:67
  142.6 1.0 fusion.11
  143.6 4.4 fusion.5
  148.7 3.3 all-to-all-start
  152.1 2.9 convolution_convert_fusion.3
  155.0 4.4 all-gather.5.cloned.1.call-done
  159.4 14.2 %multiply_convert_fusion.5.clone.4 = bf16[8192,1024]{1,0:T(8,128)(2,1)S(1)} fusion(f32[8192]{0:T(1024)S(1)} %broadcast_multiply_fusion, s32[1024]{0:T(1024)S(1)} %iota_add_fusion, f32[8192]{0:T(1024)S(1)} %bitcast.31, f32[8192]{0:T(1024)S(1)} %convert_element_type.108, s32[8192]{0:T(1024)S(1)} %bitcast.30, ...), kind=kOutput, calls=%fused_computation.clone.clone.clone.clone.clone.clone.1 | convolution fusion | flops 4362600448 | bytes 22159360 | tf_op jit(solution)/shard_map/ue,ie->ui/dot_general | solution.py:108
  173.6 4.7 fusion.12
  178.6 0.8 copy-done.7
  179.3 1.2 convolution_convert_fusion.2
  180.5 4.4 fusion.6
  185.0 95.5 %all-reduce.5.cloned.1.call-done = bf16[1024,512]{0,1:T(8,128)(2,1)} async-done(((bf16[1024,512]{0,1:T(8,128)(2,1)}), bf16[1024,512]{0,1:T(8,128)(2,1)}) %all-reduce.5.cloned.1.call-update) | async-done | bytes 1048592 | tf_op jit(solution)/shard_map/psum | solution.py:137
  280.5 67.8 %psum.42 = bf16[]{:T(256)} all-reduce(bf16[]{:T(256)} %get-tuple-element.20), channel_id=1, replica_groups=mesh['row'=8,'col'=16] {'row','col'}, use_global_device_ids=true, to_apply=%region_6.7 | all-reduce | flops 1 | bytes 4 | tf_op jit(solution)/shard_map/psum | solution.py:141
  349.0 88.4 %all-reduce.9.cloned.1.call-done = (bf16[1024,512]{0,1:T(8,128)(2,1)}, bf16[512,256]{1,0:T(8,128)(2,1)}, bf16[512,256]{1,0:T(8,128)(2,1)}) async-done(((bf16[1024,512]{0,1:T(8,128)(2,1)}, bf16[512,256]{1,0:T(8,128)(2,1)}, bf16[512,256]{1,0:T(8,128)(2,1)}), (bf16[1024,512]{0,1:T(8,128)(2,1)}, bf16[512,256]{1,0:T(8,128)(2,1)}, bf16[512,256]{1,0:T(8,128)(2,1)})) %all-reduce.9.cloned.1.call-update) | async-done | bytes 1572880 | tf_op jit(solution)/shard_map/psum | solution.py:139
  437.4 1.8 convert_element_type.107
  439.2 2.6 copy.16
  441.7 1.8 convert_element_type.119
  443.5 77.3 %all-reduce.7.cloned.1.call-done = bf16[1024,512]{0,1:T(8,128)(2,1)} async-done(((bf16[1024,512]{0,1:T(8,128)(2,1)}), bf16[1024,512]{0,1:T(8,128)(2,1)}) %all-reduce.7.cloned.1.call-update) | async-done | bytes 1048592 | tf_op jit(solution)/shard_map/psum | solution.py:137
  520.8 2.6 copy.15
  (51 shorter events, 2.9 us)
Async XLA Ops:
  7.2 15.1 %copy-start = (bf16[1024,1024]{1,0:T(8,128)(2,1)S(1)}, bf16[1024,1024]{1,0:T(8,128)(2,1)}, u32[]{:S(2)}) copy-start(bf16[1024,1024]{1,0:T(8,128)(2,1)} %param.8) | copy-start | bytes 6291460
  7.2 4.7 copy-start.9
  7.2 80.0 %all-gather.3.cloned.1.call-start = ((), (), s32[]{:S(2)}) async-start(), calls=%async_computation.2 | async-start | bytes 4718592 | tf_op jit(solution)/shard_map/all_gather | solution.py:91
  10.5 1.3 copy-start.4
  11.8 1.4 copy-start.12
  13.9 134.1 %all-to-all-start.1 = ((s32[8,1,1024]{2,1,0:T(1,128)}), s32[8,1,1024]{2,1,0:T(1,128)S(1)}, u32[]{:S(2)}, u32[]{:S(2)}) async-start(s32[8,1,1024]{2,1,0:T(1,128)} %broadcast_in_dim.15), calls=%async_computation.1 | async-start | bytes 65536 | tf_op jit(solution)/shard_map/all_to_all | solution.py:17
  22.2 3.9 copy-start.8
  22.2 137.2 %all-gather.5.cloned.1.call-start = ((), (), s32[]{:S(2)}) async-start(), calls=%async_computation.5 | async-start | bytes 4718592 | tf_op jit(solution)/shard_map/all_gather | solution.py:100
  24.8 1.3 copy-start.6
  26.1 2.4 copy-start.11
  26.6 1.0 copy-start.2
  103.2 19.0 %copy-start.3 = (f32[1024,256]{0,1:T(8,128)S(1)}, f32[1024,256]{0,1:T(8,128)}, u32[]{:S(2)}) copy-start(f32[1024,256]{0,1:T(8,128)} %copy-done.2) | copy-start | bytes 3145732
  148.7 10.7 %all-to-all-start = ((f32[8,1,1024]{2,1,0:T(1,128)}), f32[8,1,1024]{2,1,0:T(1,128)S(1)}, u32[]{:S(2)}, u32[]{:S(2)}) async-start(f32[8,1,1024]{2,1,0:T(1,128)} %broadcast_in_dim.14), calls=%async_computation | async-start | bytes 65536 | tf_op jit(solution)/shard_map/all_to_all | solution.py:17
  152.0 128.4 %all-reduce.5.cloned.1.call-start = ((), (), s32[]{:S(2)}) async-start(), calls=%async_computation.3 | async-start | bytes 2097152 | tf_op jit(solution)/shard_map/psum | solution.py:137
  155.0 282.4 %all-reduce.9.cloned.1.call-start = ((), (), s32[]{:S(2)}) async-start(), calls=%async_computation.6 | async-start | bytes 3145728 | tf_op jit(solution)/shard_map/psum | solution.py:139
  159.4 14.2 %copy-start.13 = (bf16[8192,256]{0,1:T(8,128)(2,1)S(1)}, bf16[8192,256]{0,1:T(8,128)(2,1)}, u32[]{:S(2)}) copy-start(bf16[8192,256]{0,1:T(8,128)(2,1)} %all-gather.5.cloned.1.call-done) | copy-start | bytes 12582916
  173.6 5.7 %copy-start.5 = (f32[1024,512]{1,0:T(8,128)S(1)}, f32[1024,512]{1,0:T(8,128)}, u32[]{:S(2)}) copy-start(f32[1024,512]{1,0:T(8,128)} %copy-done.4) | copy-start | bytes 6291460
  178.3 2.2 copy-start.10
  178.5 0.8 copy-start.7
  184.9 335.9 %all-reduce.7.cloned.1.call-start = ((), (), s32[]{:S(2)}) async-start(), calls=%async_computation.4 | async-start | bytes 2097152 | tf_op jit(solution)/shard_map/psum | solution.py:137
  280.5 242.9 %copy-start.1 = (bf16[1024,1024]{1,0:T(8,128)(2,1)S(1)}, bf16[1024,1024]{1,0:T(8,128)(2,1)}, u32[]{:S(2)}) copy-start(bf16[1024,1024]{1,0:T(8,128)(2,1)} %param.8) | copy-start | bytes 6291460
Sparse Core Ops, SparseCore 0:
  13.4 73.7 all-gather.2
  90.1 69.2 all-gather.4
  161.9 118.5 all-reduce.4
  285.9 151.4 all-reduce.8
  439.7 80.9 all-reduce.6
